TPU v7x, 32 devices: a whole 2x2x4 slice. The times are simulated.
32 devices in a mesh: seq: 16 (over z, y, x), head: 2 (over core).
Axes of the slice: x: 2, y: 2, z: 4, core: 2. Of those that a mesh axis runs over, the one named last changes fastest.
Arguments:
- queries: bfloat16 [2048, 2048], P('seq', 'head'), may hold values from -6 to 6
- keys: bfloat16 [2048, 512], P('seq', 'head'), may hold values from -6 to 6
- values: bfloat16 [2048, 512], P('seq', 'head'), may hold values from -6 to 6
- tile_mask: int32 [32, 32], replicated, may hold values from 0 to 1, as said below
- out_weight: bfloat16 [2048, 4096], P('head'), may hold values from -0.5 to 0.5
Outputs:
- mixed: bfloat16 [2048, 4096], P(('seq', 'head'))
Inputs may be any that keep to these rules, and one draw needn't show every extreme that they name: tile_mask[i, j] is 1 for i == j, 0 for j > i, and 0 or 1 below the diagonal.
All inputs are finite; a program needn't handle non-finite values.
Results may differ from a plain program's by a relative error of at most 0.01.
Values may be sent and summed in bfloat16 or wider, within the bound.
No kernel may reach another device: no remote copies, remote signals or barrier semaphores. Data moves between devices by JAX's collectives and lax.ppermute only.
A program may use at most 128 MiB of HBM per device.

v0:
```python
import math
import jax
import jax.numpy as jnp
from jax import lax
from jax.sharding import PartitionSpec as P

HD = 128
TILE = 64
MASK_FLOOR = -1e30


def per_device(queries, keys, values, tile_mask, out_weight):
    row_count = queries.shape[0]
    local_groups = keys.shape[1] // HD
    group = queries.shape[1] // HD // local_groups
    scale = 1.0 / math.sqrt(HD)
    seq_place = lax.axis_index("seq")
    query_index = seq_place * row_count + jnp.arange(row_count, dtype=jnp.int32)
    query_block = queries.reshape(row_count, local_groups, group, HD)
    query_tiles = query_index[::TILE] // TILE
    mask_rows = jnp.take(tile_mask, query_tiles, axis=0)

    def block_step(state, key_part, value_part, key_start):
        width = key_part.shape[0]
        key_index = key_start + jnp.arange(width, dtype=jnp.int32)
        tile_open = jnp.repeat(jnp.take(mask_rows, key_index // TILE, axis=1) > 0, TILE, axis=0)
        allowed = tile_open & (key_index[None, :] <= query_index[:, None])
        best, total, running = state
        allowed_wide = allowed[:, None, None, :]
        scores = (
            jnp.einsum(
                "qgrd,kgd->qgrk",
                query_block,
                key_part.reshape(width, local_groups, HD),
                preferred_element_type=jnp.float32,
            )
            * scale
        )
        masked = jnp.where(allowed_wide, scores, MASK_FLOOR)
        new_best = jnp.maximum(best, jnp.max(masked, axis=-1))
        weights = jnp.where(allowed_wide, jnp.exp(masked - new_best[..., None]), 0.0)
        rescale = jnp.exp(best - new_best)
        total = total * rescale + jnp.sum(weights, axis=-1)
        product = jnp.einsum(
            "qgrk,kgd->qgrd",
            weights.astype(jnp.bfloat16),
            value_part.reshape(width, local_groups, HD),
            preferred_element_type=jnp.float32,
        )
        running = running * rescale[..., None] + product
        return (new_best, total, running)

    initial = (
        jnp.full((row_count, local_groups, group), MASK_FLOOR, jnp.float32),
        jnp.zeros((row_count, local_groups, group), jnp.float32),
        jnp.zeros((row_count, local_groups, group, HD), jnp.float32),
    )
    carry = initial
    key_piece = lax.all_gather(keys, "seq", axis=0, tiled=True)
    value_piece = lax.all_gather(values, "seq", axis=0, tiled=True)
    width = key_piece.shape[0]
    block_size = math.gcd(width, 2048)
    count = width // block_size
    key_blocks = key_piece.reshape(count, block_size, key_piece.shape[1])
    value_blocks = value_piece.reshape(count, block_size, value_piece.shape[1])
    offsets = block_size * jnp.arange(count, dtype=jnp.int32)

    def advance(state, item):
        key_part, value_part, key_start = item
        return (block_step(state, key_part, value_part, key_start), None)

    carry, unused = lax.scan(advance, carry, (key_blocks, value_blocks, offsets))
    best, total, running = carry
    attended = (
        (running / total[..., None])
        .reshape(row_count, local_groups * group * HD)
        .astype(jnp.bfloat16)
    )
    return lax.psum_scatter(
        jnp.dot(attended, out_weight, preferred_element_type=jnp.float32).astype(jnp.bfloat16),
        "head",
        scatter_dimension=0,
        tiled=True,
    )


def solution(mesh):
    placed = (P("seq", "head"), P("seq", "head"), P("seq", "head"), P(), P("head", None))
    return jax.shard_map(
        per_device, mesh=mesh, in_specs=placed, out_specs=P(("seq", "head"), None), check_vma=False
    )
```

profile of v0, /device:TPU:0, one launch (start us, length us, event | category | flops | bytes accessed | tf_op | source)
XLA Modules:
  0.0 147.7 jit_solution(15410946941550882141)
XLA Ops:
  6.5 0.0 copy-start
  6.5 0.0 all-gather.3.cloned.1.call-start
  6.5 1.6 %copy.13 = bf16[128,256]{0,1:T(8,128)(2,1)} copy(bf16[128,256]{1,0:T(8,128)(2,1)} %param.6) | data formatting | bytes 131072 | tf_op args[1]
  8.1 0.0 all-gather.3.cloned.1.call-update
  8.1 0.0 all-gather.5.cloned.1.call-start
  8.2 0.7 all-gather.5.cloned.1.call-update
  8.9 0.0 reduce-scatter.2.cloned.1.call-start
  9.0 0.1 slice.3
  9.1 0.0 copy-done
  9.1 0.6 gather_fusion
  9.7 0.1 broadcast_select_fusion
  9.8 0.1 copy.10
  9.9 5.5 %gather_fusion.1 = s32[2048,2]{1,0:T(8,128)S(1)} fusion(s32[2,32]{0,1:T(8,128)S(1)} %copy.10, s32[2048]{0:T(1024)S(1)} %broadcast_clamp_fusion), kind=kCustom, calls=%fused_computation.1 | custom fusion | bytes 40960 | tf_op jit(solution)/shard_map/while/body/eval_jaxpr/jit(_take)/gather | solution.py:26
  15.3 0.3 fusion.13
  15.7 0.4 copy.11
  16.0 0.3 fusion.12
  16.3 0.5 copy.12
  16.7 1.1 reshape.123
  17.9 46.3 %all-gather.3.cloned.1.call-done = bf16[2048,256]{0,1:T(8,128)(2,1)} async-done(((bf16[128,256]{0,1:T(8,128)(2,1)}), bf16[2048,256]{0,1:T(8,128)(2,1)}) %all-gather.3.cloned.1.call-update) | async-done | bytes 1048592 | tf_op jit(solution)/shard_map/all_gather | solution.py:59
  64.2 2.7 %fusion = (f32[128,2,4]{0,2,1:T(4,128)S(1)}, f32[2,2048,128,4]{2,1,3,0:T(8,128)S(1)}) fusion(pred[128,2048]{0,1:T(8,128)(4,1)S(1)} %copy.12, bf16[2048,2,128,1]{0,2,3,1:T(8,128)(2,1)} %bitcast.47, bf16[128,2,4,128]{3,2,1,0:T(4,128)(2,1)S(1)} %reshape.123), kind=kOutput, calls=%fused_computation.4 | convolution fusion | flops 543161344 | bytes 9965568 | tf_op jit(solution)/shard_map/while/body/eval_jaxpr/qgrd,kgd->qgrk/dot_general | solution.py:31
  66.9 0.0 copy-start.1
  66.9 3.2 %copy-done.1 = f32[2,2048,128,4]{2,1,3,0:T(8,128)} copy-done((f32[2,2048,128,4]{2,1,3,0:T(8,128)}, f32[2,2048,128,4]{2,1,3,0:T(8,128)S(1)}, u32[]{:S(2)}) %copy-start.1) | copy-done | bytes 8388632
  70.1 2.0 %fusion.1 = f32[128,2,4]{0,2,1:T(4,128)S(1)} fusion(f32[2,2048,128,4]{2,1,3,0:T(8,128)S(1)} %get-tuple-element.26, f32[128,2,4]{0,2,1:T(4,128)S(1)} %broadcast_maximum_fusion, pred[128,2048]{0,1:T(8,128)(4,1)S(1)} %copy.12), kind=kLoop, calls=%fused_computation.5 | loop fusion | flops 10484736 | bytes 8658944 | tf_op jit(solution)/shard_map/while/body/eval_jaxpr/reduce_sum | solution.py:43
  72.2 48.9 %all-gather.5.cloned.1.call-done = bf16[2048,256]{1,0:T(8,128)(2,1)} async-done(((bf16[128,256]{1,0:T(8,128)(2,1)}), bf16[2048,256]{1,0:T(8,128)(2,1)}) %all-gather.5.cloned.1.call-update) | async-done | bytes 1048592 | tf_op jit(solution)/shard_map/all_gather | solution.py:60
  121.1 1.5 %copy.16 = bf16[2048,256]{0,1:T(8,128)(2,1)S(1)} copy(bf16[2048,256]{1,0:T(8,128)(2,1)} %all-gather.5.cloned.1.call-done) | data formatting | bytes 2097152 | tf_op jit(solution)/shard_map/all_gather | solution.py:60
  122.6 5.5 %fusion.17 = bf16[128,2,4,128]{0,3,2,1:T(8,128)(2,1)S(1)} fusion(bf16[2048,2,128,1]{0,2,3,1:T(8,128)(2,1)S(1)} %bitcast.48, f32[2,2048,128,4]{2,1,3,0:T(8,128)} %copy-done.1, f32[128,2,4]{0,2,1:T(4,128)S(1)} %broadcast_maximum_fusion, pred[128,2048]{0,1:T(8,128)(4,1)S(1)} %copy.12, f32[128,2,4]{0,2,1:T(4,128)S(1)} %get-tuple-element.24, ...), kind=kOutput, calls=%fused_computation.17 | convolution fusion | flops 547749888 | bytes 9973760 | tf_op jit(solution)/shard_map/while/body/eval_jaxpr/qgrk,kgd->qgrd/dot_general | solution.py:44
  128.1 5.6 %convolution_convert_fusion = bf16[128,4096]{1,0:T(8,128)(2,1)} fusion(bf16[128,1024]{0,1:T(8,128)(2,1)S(1)} %bitcast.49, bf16[1024,4096]{1,0:T(8,128)(2,1)} %param.9), kind=kOutput, calls=%fused_computation.7 | convolution fusion | flops 1074266112 | bytes 9699328 | tf_op jit(solution)/shard_map/dot_general | solution.py:80
  133.7 0.0 reduce-scatter.2.cloned.1.call-update
  133.8 7.4 %reduce-scatter.2.cloned.1.call-done = bf16[64,4096]{1,0:T(8,128)(2,1)} async-done(((bf16[128,4096]{1,0:T(8,128)(2,1)}), bf16[64,4096]{1,0:T(8,128)(2,1)}) %reduce-scatter.2.cloned.1.call-update) | async-done | bytes 524304 | tf_op jit(solution)/shard_map/reduce_scatter | solution.py:79
  (8 shorter events, 0.1 us)
Async XLA Ops:
  6.5 2.6 %copy-start = (s32[32,32]{1,0:T(8,128)S(1)}, s32[32,32]{1,0:T(8,128)}, u32[]{:S(2)}) copy-start(s32[32,32]{1,0:T(8,128)} %param.8) | copy-start | bytes 12292
  6.5 57.6 %all-gather.3.cloned.1.call-start = ((), (), s32[]{:S(2)}) async-start(), calls=%async_computation.1 | async-start | bytes 1114112 | tf_op jit(solution)/shard_map/all_gather | solution.py:59
  8.1 112.9 %all-gather.5.cloned.1.call-start = ((), (), s32[]{:S(2)}) async-start(), calls=%async_computation.2 | async-start | bytes 1114112 | tf_op jit(solution)/shard_map/all_gather | solution.py:60
  8.9 132.2 %reduce-scatter.2.cloned.1.call-start = ((), (), s32[]{:S(2)}) async-start(), calls=%async_computation.3 | async-start | bytes 1572864 | tf_op jit(solution)/shard_map/reduce_scatter | solution.py:79
  66.9 3.2 %copy-start.1 = (f32[2,2048,128,4]{2,1,3,0:T(8,128)}, f32[2,2048,128,4]{2,1,3,0:T(8,128)S(1)}, u32[]{:S(2)}) copy-start(f32[2,2048,128,4]{2,1,3,0:T(8,128)S(1)} %get-tuple-element.26) | copy-start | bytes 25165828
Sparse Core Ops, SparseCore 0:
  10.0 54.0 all-gather.2
  66.9 54.0 all-gather.4
  133.9 7.2 reduce-scatter.1
where the time goes:
time: 148 us
  waiting for transfers between devices  103 us (70%)
  local copies, waits for them, and re-layouts  14.4 us (10%)
  matrix products  13.9 us (9%)
  between operations  13.2 us (9%)
  other arithmetic  2.75 us (2%)
    all_gather x1, waiting for transfers between devices, per_device(): value_piece = lax.all_gather(values, 'seq', axis=0, tiled=True)  48.9 us
    all_gather x1, waiting for transfers between devices, per_device(): key_piece = lax.all_gather(keys, 'seq', axis=0, tiled=True)  46.3 us
    reduce_scatter x1, waiting for transfers between devices, per_device(): lax.psum_scatter(jnp.dot(attended, out_weight, preferred_element_type=jnp...  7.38 us
    dot_general x1, matrix products, per_device(): jnp.dot(attended, out_weight, preferred_element_type=jnp.float32)  5.64 us
    dot_general x1, matrix products, block_step(): jnp.einsum('qgrk,kgd->qgrd', weights.astype(jnp.bfloat16), value_part.res...  5.52 us
    gather x1, local copies, waits for them, and re-layouts, block_step(): jnp.take(mask_rows, key_index // TILE, axis=1) > 0  5.46 us
    unnamed x5, local copies, waits for them, and re-layouts  4.8 us
  transfers between devices with their start and end apart: 3, of which 3 were waited for; matrix products, arithmetic and copies ran while one was open for 9% of the time, Pallas kernels for 0%

commit v1 on v0

--- a/solution.py
+++ b/solution.py
@@ -57,7 +57,12 @@
     )
     carry = initial
     key_piece = lax.all_gather(keys, "seq", axis=0, tiled=True)
-    value_piece = lax.all_gather(values, "seq", axis=0, tiled=True)
+    ring = [values]
+    for hop in range(15):
+        ring.append(lax.ppermute(ring[-1], "seq", [(dev, (dev + 1) % 16) for dev in range(16)]))
+    value_piece = jnp.roll(
+        jnp.concatenate(ring[::-1], axis=0), (lax.axis_index("seq") + 1) * ring[0].shape[0], axis=0
+    )
     width = key_piece.shape[0]
     block_size = math.gcd(width, 2048)
     count = width // block_size

time: 148 us -> 153 us (1.034)
  waiting for transfers between devices: 103 us -> 115 us
  matrix products: 13.9 us -> 7.16 us
  local copies, waits for them, and re-layouts: 14.4 us -> 10.7 us
  starting transfers between devices: 0.08 us -> 3.05 us
    ppermute x0 -> x15, waiting for transfers between devices: none -> 110 us  [per_device(): lax.ppermute(ring[-1], 'seq', [(dev, (dev + 1) % 16) for dev in range(16)])]
    all_gather x1 -> x0, waiting for transfers between devices: 48.9 us -> none  [per_device(): value_piece = lax.all_gather(values, 'seq', axis=0, tiled=True)]
    all_gather x1, waiting for transfers between devices: 46.3 us -> 0.02 us  [per_device(): key_piece = lax.all_gather(keys, 'seq', axis=0, tiled=True)]
    dot_general x1, matrix products: 5.52 us -> 2.14 us  [block_step(): jnp.einsum('qgrk,kgd->qgrd', weights.astype(jnp.bfloat16), value_part.res...]
    dot_general x1, matrix products: 5.64 us -> 2.27 us  [per_device(): jnp.dot(attended, out_weight, preferred_element_type=jnp.float32)]
    ppermute x0 -> x15, starting transfers between devices: none -> 3 us  [per_device(): lax.ppermute(ring[-1], 'seq', [(dev, (dev + 1) % 16) for dev in range(16)])]
    unnamed x5 -> x40, local copies, waits for them, and re-layouts: 4.8 us -> 1.86 us
    reduce_scatter x1, waiting for transfers between devices: 7.38 us -> 4.66 us  [per_device(): lax.psum_scatter(jnp.dot(attended, out_weight, preferred_element_type=jnp...]
  transfers between devices with their start and end apart: 3 -> 17, of which waited for: 3 -> 16; matrix products, arithmetic and copies ran while one was open for 9% -> 7% of each run, Pallas kernels for 0% -> 0%
where the time goes in v1:
time: 153 us
  waiting for transfers between devices  115 us (75%)
  between operations  13.8 us (9%)
  local copies, waits for them, and re-layouts  10.7 us (7%)
  matrix products  7.16 us (5%)
  starting transfers between devices  3.05 us (2%)
  other arithmetic  2.74 us (2%)
    ppermute x15, waiting for transfers between devices, per_device(): lax.ppermute(ring[-1], 'seq', [(dev, (dev + 1) % 16) for dev in range(16)])  110 us
    gather x1, local copies, waits for them, and re-layouts, block_step(): jnp.take(mask_rows, key_index // TILE, axis=1) > 0  5.46 us
    reduce_scatter x1, waiting for transfers between devices, per_device(): lax.psum_scatter(jnp.dot(attended, out_weight, preferred_element_type=jnp...  4.66 us
  transfers between devices with their start and end apart: 17, of which 16 were waited for; matrix products, arithmetic and copies ran while one was open for 7% of the time, Pallas kernels for 0%

profile of v1, /device:TPU:0, one launch (start us, length us, event | category | flops | bytes accessed | tf_op | source)
XLA Modules:
  0.0 152.5 jit_solution(5617468430861336470)
XLA Ops:
  6.5 3.0 %collective-permute-start = (bf16[128,256]{1,0:T(8,128)(2,1)}, bf16[128,256]{1,0:T(8,128)(2,1)S(1)}, u32[]{:S(2)}, u32[]{:S(2)}) collective-permute-start(bf16[128,256]{1,0:T(8,128)(2,1)} %param.7), channel_id=1, source_target_pairs={{0,2},{2,4},{4,6},{6,8},{8,10},{10,12},{12,14},{14,16},{16,18},{18... | collective-permute-start | bytes 196616 | tf_op jit(solution)/shard_map/ppermute | solution.py:62
  9.5 6.4 %collective-permute-done = bf16[128,256]{1,0:T(8,128)(2,1)S(1)} collective-permute-done((bf16[128,256]{1,0:T(8,128)(2,1)}, bf16[128,256]{1,0:T(8,128)(2,1)S(1)}, u32[]{:S(2)}, u32[]{:S(2)}) %collective-permute-start) | collective-permute-done | bytes 65568 | tf_op jit(solution)/shard_map/ppermute | solution.py:62
  16.0 7.9 %collective-permute-done.1 = bf16[128,256]{1,0:T(8,128)(2,1)S(1)} collective-permute-done((bf16[128,256]{1,0:T(8,128)(2,1)S(1)}, bf16[128,256]{1,0:T(8,128)(2,1)S(1)}, u32[]{:S(2)}, u32[]{:S(2)}) %collective-permute-start.1) | collective-permute-done | bytes 65568 | tf_op jit(solution)/shard_map/ppermute | solution.py:62
  23.8 0.0 collective-permute-start.2
  23.8 7.9 %collective-permute-done.2 = bf16[128,256]{1,0:T(8,128)(2,1)S(1)} collective-permute-done((bf16[128,256]{1,0:T(8,128)(2,1)S(1)}, bf16[128,256]{1,0:T(8,128)(2,1)S(1)}, u32[]{:S(2)}, u32[]{:S(2)}) %collective-permute-start.2) | collective-permute-done | bytes 65568 | tf_op jit(solution)/shard_map/ppermute | solution.py:62
  31.7 0.0 collective-permute-start.3
  31.7 7.9 %collective-permute-done.3 = bf16[128,256]{1,0:T(8,128)(2,1)S(1)} collective-permute-done((bf16[128,256]{1,0:T(8,128)(2,1)S(1)}, bf16[128,256]{1,0:T(8,128)(2,1)S(1)}, u32[]{:S(2)}, u32[]{:S(2)}) %collective-permute-start.3) | collective-permute-done | bytes 65568 | tf_op jit(solution)/shard_map/ppermute | solution.py:62
  39.5 0.0 collective-permute-start.4
  39.5 7.9 %collective-permute-done.4 = bf16[128,256]{1,0:T(8,128)(2,1)S(1)} collective-permute-done((bf16[128,256]{1,0:T(8,128)(2,1)S(1)}, bf16[128,256]{1,0:T(8,128)(2,1)S(1)}, u32[]{:S(2)}, u32[]{:S(2)}) %collective-permute-start.4) | collective-permute-done | bytes 65568 | tf_op jit(solution)/shard_map/ppermute | solution.py:62
  47.4 8.4 %collective-permute-done.5 = bf16[128,256]{1,0:T(8,128)(2,1)S(1)} collective-permute-done((bf16[128,256]{1,0:T(8,128)(2,1)S(1)}, bf16[128,256]{1,0:T(8,128)(2,1)S(1)}, u32[]{:S(2)}, u32[]{:S(2)}) %collective-permute-start.5) | collective-permute-done | bytes 65568 | tf_op jit(solution)/shard_map/ppermute | solution.py:62
  55.9 0.0 collective-permute-start.6
  55.9 1.6 %copy.13 = bf16[128,256]{0,1:T(8,128)(2,1)} copy(bf16[128,256]{1,0:T(8,128)(2,1)} %param.6) | data formatting | bytes 131072 | tf_op args[1]
  57.4 0.0 all-gather.2.cloned.1.call-update
  57.5 0.0 reduce-scatter.2.cloned.1.call-start
  57.5 6.2 %collective-permute-done.6 = bf16[128,256]{1,0:T(8,128)(2,1)S(1)} collective-permute-done((bf16[128,256]{1,0:T(8,128)(2,1)S(1)}, bf16[128,256]{1,0:T(8,128)(2,1)S(1)}, u32[]{:S(2)}, u32[]{:S(2)}) %collective-permute-start.6) | collective-permute-done | bytes 65568 | tf_op jit(solution)/shard_map/ppermute | solution.py:62
  63.7 0.0 collective-permute-start.7
  63.7 7.9 %collective-permute-done.7 = bf16[128,256]{1,0:T(8,128)(2,1)S(1)} collective-permute-done((bf16[128,256]{1,0:T(8,128)(2,1)S(1)}, bf16[128,256]{1,0:T(8,128)(2,1)S(1)}, u32[]{:S(2)}, u32[]{:S(2)}) %collective-permute-start.7) | collective-permute-done | bytes 65568 | tf_op jit(solution)/shard_map/ppermute | solution.py:62
  71.6 0.0 collective-permute-start.8
  71.7 7.9 %collective-permute-done.8 = bf16[128,256]{1,0:T(8,128)(2,1)S(1)} collective-permute-done((bf16[128,256]{1,0:T(8,128)(2,1)S(1)}, bf16[128,256]{1,0:T(8,128)(2,1)S(1)}, u32[]{:S(2)}, u32[]{:S(2)}) %collective-permute-start.8) | collective-permute-done | bytes 65568 | tf_op jit(solution)/shard_map/ppermute | solution.py:62
  79.5 0.1 slice.3
  79.6 7.9 %collective-permute-done.9 = bf16[128,256]{1,0:T(8,128)(2,1)S(1)} collective-permute-done((bf16[128,256]{1,0:T(8,128)(2,1)S(1)}, bf16[128,256]{1,0:T(8,128)(2,1)S(1)}, u32[]{:S(2)}, u32[]{:S(2)}) %collective-permute-start.9) | collective-permute-done | bytes 65568 | tf_op jit(solution)/shard_map/ppermute | solution.py:62
  87.6 7.8 %collective-permute-done.10 = bf16[128,256]{1,0:T(8,128)(2,1)S(1)} collective-permute-done((bf16[128,256]{1,0:T(8,128)(2,1)S(1)}, bf16[128,256]{1,0:T(8,128)(2,1)S(1)}, u32[]{:S(2)}, u32[]{:S(2)}) %collective-permute-start.10) | collective-permute-done | bytes 65568 | tf_op jit(solution)/shard_map/ppermute | solution.py:62
  95.4 0.6 gather_fusion
  96.0 9.0 %collective-permute-done.11 = bf16[128,256]{1,0:T(8,128)(2,1)S(1)} collective-permute-done((bf16[128,256]{1,0:T(8,128)(2,1)S(1)}, bf16[128,256]{1,0:T(8,128)(2,1)S(1)}, u32[]{:S(2)}, u32[]{:S(2)}) %collective-permute-start.11) | collective-permute-done | bytes 65568 | tf_op jit(solution)/shard_map/ppermute | solution.py:62
  105.0 0.1 broadcast_select_fusion
  105.1 0.1 copy.10
  105.2 5.5 %gather_fusion.1 = s32[2048,2]{1,0:T(8,128)S(1)} fusion(s32[2,32]{0,1:T(8,128)S(1)} %copy.10, s32[2048]{0:T(1024)S(1)} %broadcast_clamp_fusion), kind=kCustom, calls=%fused_computation.1 | custom fusion | bytes 40960 | tf_op jit(solution)/shard_map/while/body/eval_jaxpr/jit(_take)/gather | solution.py:26
  110.6 4.1 %collective-permute-done.12 = bf16[128,256]{1,0:T(8,128)(2,1)S(1)} collective-permute-done((bf16[128,256]{1,0:T(8,128)(2,1)S(1)}, bf16[128,256]{1,0:T(8,128)(2,1)S(1)}, u32[]{:S(2)}, u32[]{:S(2)}) %collective-permute-start.12) | collective-permute-done | bytes 65568 | tf_op jit(solution)/shard_map/ppermute | solution.py:62
  114.7 7.9 %collective-permute-done.13 = bf16[128,256]{1,0:T(8,128)(2,1)S(1)} collective-permute-done((bf16[128,256]{1,0:T(8,128)(2,1)S(1)}, bf16[128,256]{1,0:T(8,128)(2,1)S(1)}, u32[]{:S(2)}, u32[]{:S(2)}) %collective-permute-start.13) | collective-permute-done | bytes 65568 | tf_op jit(solution)/shard_map/ppermute | solution.py:62
  122.6 0.3 fusion.13
  122.9 0.0 copy-start.1
  123.0 1.1 reshape.123
  124.1 0.4 copy.11
  124.5 0.3 fusion.12
  124.7 0.5 copy.12
  125.2 5.3 %collective-permute-done.14 = bf16[128,256]{1,0:T(8,128)(2,1)S(1)} collective-permute-done((bf16[128,256]{1,0:T(8,128)(2,1)S(1)}, bf16[128,256]{1,0:T(8,128)(2,1)S(1)}, u32[]{:S(2)}, u32[]{:S(2)}) %collective-permute-start.14) | collective-permute-done | bytes 65568 | tf_op jit(solution)/shard_map/ppermute | solution.py:62
  130.9 0.1 constant_dynamic-slice_fusion
  131.0 0.6 copy.16
  131.7 0.0 all-gather.2.cloned.1.call-done
  131.7 2.7 %fusion = (f32[128,2,4]{0,2,1:T(4,128)S(1)}, f32[2,2048,128,4]{2,1,3,0:T(8,128)S(1)}) fusion(pred[128,2048]{0,1:T(8,128)(4,1)S(1)} %copy.12, bf16[2048,2,128,1]{0,2,3,1:T(8,128)(2,1)} %bitcast.49, bf16[128,2,4,128]{3,2,1,0:T(4,128)(2,1)S(1)} %reshape.123), kind=kOutput, calls=%fused_computation.4 | convolution fusion | flops 543161344 | bytes 9965568 | tf_op jit(solution)/shard_map/while/body/eval_jaxpr/qgrd,kgd->qgrk/dot_general | solution.py:31
  134.4 0.0 slice-start
  134.5 2.0 %fusion.1 = f32[128,2,4]{0,2,1:T(4,128)S(1)} fusion(f32[2,2048,128,4]{2,1,3,0:T(8,128)S(1)} %get-tuple-element.26, f32[128,2,4]{0,2,1:T(4,128)S(1)} %broadcast_maximum_fusion, pred[128,2048]{0,1:T(8,128)(4,1)S(1)} %copy.12), kind=kLoop, calls=%fused_computation.5 | loop fusion | flops 10484736 | bytes 8658944 | tf_op jit(solution)/shard_map/while/body/eval_jaxpr/reduce_sum | solution.py:43
  136.5 0.0 slice-start.1
  136.5 2.1 %fusion.17 = bf16[128,2,4,128]{0,3,2,1:T(8,128)(2,1)S(1)} fusion(bf16[2048,2,128,1]{0,2,3,1:T(8,128)(2,1)S(1)} %bitcast.50, f32[2,2048,128,4]{2,1,3,0:T(8,128)S(1)} %get-tuple-element.26, f32[128,2,4]{0,2,1:T(4,128)S(1)} %broadcast_maximum_fusion, pred[128,2048]{0,1:T(8,128)(4,1)S(1)} %copy.12, f32[128,2,4]{0,2,1:T(4,128)S(1)} %get-tuple-element.24, ...), kind=kOutput, calls=%fused_computation.17 | convolution fusion | flops 547749888 | bytes 9973760 | tf_op jit(solution)/shard_map/while/body/eval_jaxpr/qgrk,kgd->qgrd/dot_general | solution.py:44
  138.7 0.1 slice-done.1
  138.7 2.3 %convolution_convert_fusion = bf16[128,4096]{1,0:T(8,128)(2,1)} fusion(bf16[128,1024]{0,1:T(8,128)(2,1)S(1)} %bitcast.51, bf16[1024,4096]{1,0:T(8,128)(2,1)S(1)} %bitcast.48), kind=kOutput, calls=%fused_computation.7 | convolution fusion | flops 1074266112 | bytes 9699328 | tf_op jit(solution)/shard_map/dot_general | solution.py:85
  141.0 0.0 reduce-scatter.2.cloned.1.call-update
  141.0 4.7 %reduce-scatter.2.cloned.1.call-done = bf16[64,4096]{1,0:T(8,128)(2,1)} async-done(((bf16[128,4096]{1,0:T(8,128)(2,1)}), bf16[64,4096]{1,0:T(8,128)(2,1)}) %reduce-scatter.2.cloned.1.call-update) | async-done | bytes 524304 | tf_op jit(solution)/shard_map/reduce_scatter | solution.py:84
  (54 shorter events, 0.3 us)
Async XLA Ops:
  6.5 88.9 %copy-start = (s32[32,32]{1,0:T(8,128)S(1)}, s32[32,32]{1,0:T(8,128)}, u32[]{:S(2)}) copy-start(s32[32,32]{1,0:T(8,128)} %param.8) | copy-start | bytes 12292
  6.5 125.1 %all-gather.2.cloned.1.call-start = ((), (), s32[]{:S(2)}) async-start(), calls=%async_computation.1 | async-start | bytes 1114112 | tf_op jit(solution)/shard_map/all_gather | solution.py:59
  6.5 9.4 %collective-permute-start = (bf16[128,256]{1,0:T(8,128)(2,1)}, bf16[128,256]{1,0:T(8,128)(2,1)S(1)}, u32[]{:S(2)}, u32[]{:S(2)}) collective-permute-start(bf16[128,256]{1,0:T(8,128)(2,1)} %param.7), channel_id=1, source_target_pairs={{0,2},{2,4},{4,6},{6,8},{8,10},{10,12},{12,14},{14,16},{16,18},{18... | collective-permute-start | bytes 196616 | tf_op jit(solution)/shard_map/ppermute | solution.py:62
  16.0 7.9 %collective-permute-start.1 = (bf16[128,256]{1,0:T(8,128)(2,1)S(1)}, bf16[128,256]{1,0:T(8,128)(2,1)S(1)}, u32[]{:S(2)}, u32[]{:S(2)}) collective-permute-start(bf16[128,256]{1,0:T(8,128)(2,1)S(1)} %collective-permute-done), channel_id=1, source_target_pairs={{0,2},{2,4},{4,6},{6,8},{8,10},{10,12},{12,14},{14,16},{16,18},{18... | collective-permute-start | bytes 196616 | tf_op jit(solution)/shard_map/ppermute | solution.py:62
  23.8 7.9 %collective-permute-start.2 = (bf16[128,256]{1,0:T(8,128)(2,1)S(1)}, bf16[128,256]{1,0:T(8,128)(2,1)S(1)}, u32[]{:S(2)}, u32[]{:S(2)}) collective-permute-start(bf16[128,256]{1,0:T(8,128)(2,1)S(1)} %collective-permute-done.1), channel_id=1, source_target_pairs={{0,2},{2,4},{4,6},{6,8},{8,10},{10,12},{12,14},{14,16},{16,18},{18... | collective-permute-start | bytes 196616 | tf_op jit(solution)/shard_map/ppermute | solution.py:62
  31.7 7.9 %collective-permute-start.3 = (bf16[128,256]{1,0:T(8,128)(2,1)S(1)}, bf16[128,256]{1,0:T(8,128)(2,1)S(1)}, u32[]{:S(2)}, u32[]{:S(2)}) collective-permute-start(bf16[128,256]{1,0:T(8,128)(2,1)S(1)} %collective-permute-done.2), channel_id=1, source_target_pairs={{0,2},{2,4},{4,6},{6,8},{8,10},{10,12},{12,14},{14,16},{16,18},{18... | collective-permute-start | bytes 196616 | tf_op jit(solution)/shard_map/ppermute | solution.py:62
  39.5 7.9 %collective-permute-start.4 = (bf16[128,256]{1,0:T(8,128)(2,1)S(1)}, bf16[128,256]{1,0:T(8,128)(2,1)S(1)}, u32[]{:S(2)}, u32[]{:S(2)}) collective-permute-start(bf16[128,256]{1,0:T(8,128)(2,1)S(1)} %collective-permute-done.3), channel_id=1, source_target_pairs={{0,2},{2,4},{4,6},{6,8},{8,10},{10,12},{12,14},{14,16},{16,18},{18... | collective-permute-start | bytes 196616 | tf_op jit(solution)/shard_map/ppermute | solution.py:62
  47.4 8.4 %collective-permute-start.5 = (bf16[128,256]{1,0:T(8,128)(2,1)S(1)}, bf16[128,256]{1,0:T(8,128)(2,1)S(1)}, u32[]{:S(2)}, u32[]{:S(2)}) collective-permute-start(bf16[128,256]{1,0:T(8,128)(2,1)S(1)} %collective-permute-done.4), channel_id=1, source_target_pairs={{0,2},{2,4},{4,6},{6,8},{8,10},{10,12},{12,14},{14,16},{16,18},{18... | collective-permute-start | bytes 196616 | tf_op jit(solution)/shard_map/ppermute | solution.py:62
  55.9 7.9 %collective-permute-start.6 = (bf16[128,256]{1,0:T(8,128)(2,1)S(1)}, bf16[128,256]{1,0:T(8,128)(2,1)S(1)}, u32[]{:S(2)}, u32[]{:S(2)}) collective-permute-start(bf16[128,256]{1,0:T(8,128)(2,1)S(1)} %collective-permute-done.5), channel_id=1, source_target_pairs={{0,2},{2,4},{4,6},{6,8},{8,10},{10,12},{12,14},{14,16},{16,18},{18... | collective-permute-start | bytes 196616 | tf_op jit(solution)/shard_map/ppermute | solution.py:62
  57.5 88.2 %reduce-scatter.2.cloned.1.call-start = ((), (), s32[]{:S(2)}) async-start(), calls=%async_computation.2 | async-start | bytes 1572864 | tf_op jit(solution)/shard_map/reduce_scatter | solution.py:84
  63.7 7.9 %collective-permute-start.7 = (bf16[128,256]{1,0:T(8,128)(2,1)S(1)}, bf16[128,256]{1,0:T(8,128)(2,1)S(1)}, u32[]{:S(2)}, u32[]{:S(2)}) collective-permute-start(bf16[128,256]{1,0:T(8,128)(2,1)S(1)} %collective-permute-done.6), channel_id=1, source_target_pairs={{0,2},{2,4},{4,6},{6,8},{8,10},{10,12},{12,14},{14,16},{16,18},{18... | collective-permute-start | bytes 196616 | tf_op jit(solution)/shard_map/ppermute | solution.py:62
  71.6 7.9 %collective-permute-start.8 = (bf16[128,256]{1,0:T(8,128)(2,1)S(1)}, bf16[128,256]{1,0:T(8,128)(2,1)S(1)}, u32[]{:S(2)}, u32[]{:S(2)}) collective-permute-start(bf16[128,256]{1,0:T(8,128)(2,1)S(1)} %collective-permute-done.7), channel_id=1, source_target_pairs={{0,2},{2,4},{4,6},{6,8},{8,10},{10,12},{12,14},{14,16},{16,18},{18... | collective-permute-start | bytes 196616 | tf_op jit(solution)/shard_map/ppermute | solution.py:62
  79.5 8.0 %collective-permute-start.9 = (bf16[128,256]{1,0:T(8,128)(2,1)S(1)}, bf16[128,256]{1,0:T(8,128)(2,1)S(1)}, u32[]{:S(2)}, u32[]{:S(2)}) collective-permute-start(bf16[128,256]{1,0:T(8,128)(2,1)S(1)} %collective-permute-done.8), channel_id=1, source_target_pairs={{0,2},{2,4},{4,6},{6,8},{8,10},{10,12},{12,14},{14,16},{16,18},{18... | collective-permute-start | bytes 196616 | tf_op jit(solution)/shard_map/ppermute | solution.py:62
  87.5 7.9 %collective-permute-start.10 = (bf16[128,256]{1,0:T(8,128)(2,1)S(1)}, bf16[128,256]{1,0:T(8,128)(2,1)S(1)}, u32[]{:S(2)}, u32[]{:S(2)}) collective-permute-start(bf16[128,256]{1,0:T(8,128)(2,1)S(1)} %collective-permute-done.9), channel_id=1, source_target_pairs={{0,2},{2,4},{4,6},{6,8},{8,10},{10,12},{12,14},{14,16},{16,18},{18... | collective-permute-start | bytes 196616 | tf_op jit(solution)/shard_map/ppermute | solution.py:62
  95.4 9.6 %collective-permute-start.11 = (bf16[128,256]{1,0:T(8,128)(2,1)S(1)}, bf16[128,256]{1,0:T(8,128)(2,1)S(1)}, u32[]{:S(2)}, u32[]{:S(2)}) collective-permute-start(bf16[128,256]{1,0:T(8,128)(2,1)S(1)} %collective-permute-done.10), channel_id=1, source_target_pairs={{0,2},{2,4},{4,6},{6,8},{8,10},{10,12},{12,14},{14,16},{16,18},{18... | collective-permute-start | bytes 196616 | tf_op jit(solution)/shard_map/ppermute | solution.py:62
  105.0 9.7 %collective-permute-start.12 = (bf16[128,256]{1,0:T(8,128)(2,1)S(1)}, bf16[128,256]{1,0:T(8,128)(2,1)S(1)}, u32[]{:S(2)}, u32[]{:S(2)}) collective-permute-start(bf16[128,256]{1,0:T(8,128)(2,1)S(1)} %collective-permute-done.11), channel_id=1, source_target_pairs={{0,2},{2,4},{4,6},{6,8},{8,10},{10,12},{12,14},{14,16},{16,18},{18... | collective-permute-start | bytes 196616 | tf_op jit(solution)/shard_map/ppermute | solution.py:62
  114.7 7.9 %collective-permute-start.13 = (bf16[128,256]{1,0:T(8,128)(2,1)S(1)}, bf16[128,256]{1,0:T(8,128)(2,1)S(1)}, u32[]{:S(2)}, u32[]{:S(2)}) collective-permute-start(bf16[128,256]{1,0:T(8,128)(2,1)S(1)} %collective-permute-done.12), channel_id=1, source_target_pairs={{0,2},{2,4},{4,6},{6,8},{8,10},{10,12},{12,14},{14,16},{16,18},{18... | collective-permute-start | bytes 196616 | tf_op jit(solution)/shard_map/ppermute | solution.py:62
  122.6 7.9 %collective-permute-start.14 = (bf16[128,256]{1,0:T(8,128)(2,1)S(1)}, bf16[128,256]{1,0:T(8,128)(2,1)S(1)}, u32[]{:S(2)}, u32[]{:S(2)}) collective-permute-start(bf16[128,256]{1,0:T(8,128)(2,1)S(1)} %collective-permute-done.13), channel_id=1, source_target_pairs={{0,2},{2,4},{4,6},{6,8},{8,10},{10,12},{12,14},{14,16},{16,18},{18... | collective-permute-start | bytes 196616 | tf_op jit(solution)/shard_map/ppermute | solution.py:62
  122.9 7.7 %copy-start.1 = (bf16[128,256]{1,0:T(8,128)(2,1)S(1)}, bf16[128,256]{1,0:T(8,128)(2,1)}, u32[]{:S(2)}) copy-start(bf16[128,256]{1,0:T(8,128)(2,1)} %param.7) | copy-start | bytes 196612
  134.4 4.2 %slice-start = ((s8[8388608]{0:T(1024)(128)(4,1)}), s8[4194304]{0:T(1024)(128)(4,1)S(1)}, s32[]{:S(2)}) async-start(s8[8388608]{0:T(1024)(128)(4,1)} %bitcast.47), calls=%async_computation.3 | async-start | bytes 8388608
  136.5 2.2 %slice-start.1 = ((s8[8388608]{0:T(1024)(128)(4,1)}), s8[4194304]{0:T(1024)(128)(4,1)S(1)}, s32[]{:S(2)}) async-start(s8[8388608]{0:T(1024)(128)(4,1)} %bitcast.47), calls=%async_computation.4 | async-start | bytes 8388608
Sparse Core Ops, SparseCore 0:
  57.6 54.3 all-gather.1
  141.1 4.4 reduce-scatter.1
